TPU v7x, 32 devices: a whole 2x2x4 slice. The times are simulated.
32 devices in a mesh: row: 4 (over x, core), col: 8 (over z, y).
Axes of the slice: x: 2, y: 2, z: 4, core: 2. Of those that a mesh axis runs over, the one named last changes fastest.
Arguments:
- weight: bfloat16 [16384, 16384], P('row', 'col'), may hold values from -0.046875 to 0.046875
- momentum: float32 [16384, 16384], P('row', 'col'), may hold values from -36 to 36
- right_factor: float32 [16384, 512], P(('col', 'row')), may hold values from -0.046875 to 0.046875
- output_grads: bfloat16 [1024, 16384], P('col', 'row'), may hold values from -0.1875 to 0.1875
- activations: bfloat16 [1024, 16384], P('row', 'col'), may hold values from -6 to 6
Outputs:
- new_weight: bfloat16 [16384, 16384], P('row', 'col')
- new_momentum: float32 [16384, 16384], P('row', 'col')
- new_factor: float32 [16384, 512], P(('col', 'row'))
All inputs are finite; a program needn't handle non-finite values.
Results may differ from a plain program's by a relative error of at most 0.0004.
Values may be sent and summed in bfloat16 or wider, within the bound.
No kernel may reach another device: no remote copies, remote signals or barrier semaphores. Data moves between devices by JAX's collectives and lax.ppermute only.
A program may use at most 192 MiB of HBM per device.

v0:
```python
import math
import jax
import jax.numpy as jnp
from jax import lax
from jax.sharding import PartitionSpec as P

D_OUT = 16384
D_IN = 16384
FULL_PRECISION = lax.Precision.HIGHEST
MOMENTUM_DECAY = 0.95
LEARN_RATE = 0.002
NORM_EPS = 1e-06


def contract_rows(first, second):
    return lax.dot_general(
        first,
        second,
        (((0,), (0,)), ((), ())),
        precision=FULL_PRECISION,
        preferred_element_type=jnp.float32,
    )


def outer_rows(first, second):
    return lax.dot_general(
        first,
        second,
        (((1,), (1,)), ((), ())),
        precision=FULL_PRECISION,
        preferred_element_type=jnp.float32,
    )


def orthogonalize(left_factor, gram_matrix):
    lower_factor = jnp.linalg.cholesky(gram_matrix)
    identity = jnp.eye(gram_matrix.shape[0], dtype=gram_matrix.dtype)
    inverse = jax.scipy.linalg.solve_triangular(lower_factor, identity, lower=True)
    return outer_rows(left_factor, inverse)


def body(weight, momentum, right_factor, output_grads, activations):
    grads_whole = lax.all_gather(output_grads, "col", axis=0, tiled=True)
    grad_tile = lax.dot_general(
        grads_whole,
        lax.all_gather(activations, "row", axis=0, tiled=True),
        (((0,), (0,)), ((), ())),
        preferred_element_type=jnp.float32,
    )
    buffer = momentum + grad_tile
    factor_block = lax.all_gather(right_factor, "row", axis=0, tiled=True)
    left_partial = jnp.dot(
        buffer, factor_block, precision=FULL_PRECISION, preferred_element_type=jnp.float32
    )
    left_factor = lax.psum(left_partial, "col")
    gram_matrix = lax.psum(contract_rows(left_factor, left_factor), "row")
    ortho_left = orthogonalize(left_factor, gram_matrix)
    right_piece = lax.psum_scatter(
        contract_rows(buffer, ortho_left), "row", scatter_dimension=0, tiled=True
    )
    column_squares = lax.psum(jnp.sum(right_piece * right_piece, axis=0), ("row", "col"))
    column_norm = jnp.sqrt(column_squares + NORM_EPS)
    new_factor = right_piece / column_norm
    projected = lax.all_gather(right_piece, "row", axis=0, tiled=True)
    new_momentum = buffer - (1.0 - MOMENTUM_DECAY) * outer_rows(ortho_left, projected)
    factor_cols = projected / column_norm
    step_scale = LEARN_RATE * math.sqrt(max(D_OUT, D_IN))
    new_weight = (
        weight.astype(jnp.float32) - step_scale * outer_rows(ortho_left, factor_cols)
    ).astype(jnp.bfloat16)
    return (new_weight, new_momentum, new_factor)


def solution(mesh):
    in_specs = (
        P("row", "col"),
        P("row", "col"),
        P(("col", "row"), None),
        P("col", "row"),
        P("row", "col"),
    )
    out_specs = (P("row", "col"), P("row", "col"), P(("col", "row"), None))
    return jax.shard_map(body, mesh=mesh, in_specs=in_specs, out_specs=out_specs, check_vma=False)
```

profile of v0, /device:TPU:0, one launch (start us, length us, event | category | flops | bytes accessed | tf_op | source)
XLA Modules:
  0.0 1043.1 jit_solution(17681060143477142184)
XLA Ops:
  9.4 37.3 %all-gather.7.cloned.1.call-done = bf16[1024,2048]{1,0:T(8,128)(2,1)} async-done(((bf16[256,2048]{1,0:T(8,128)(2,1)}), bf16[1024,2048]{1,0:T(8,128)(2,1)}) %all-gather.7.cloned.1.call-update) | async-done | bytes 4194320 | tf_op jit(solution)/shard_map/all_gather | solution.py:46
  46.7 126.6 %all-gather.5.cloned.1.call-done = bf16[1024,4096]{1,0:T(8,128)(2,1)} async-done(((bf16[128,4096]{1,0:T(8,128)(2,1)}), bf16[1024,4096]{1,0:T(8,128)(2,1)}) %all-gather.5.cloned.1.call-update) | async-done | bytes 8388624 | tf_op jit(solution)/shard_map/all_gather | solution.py:43
  173.4 36.2 %convolution_add_fusion = f32[4096,2048]{1,0:T(8,128)} fusion(f32[4096,2048]{1,0:T(8,128)} %param.6, bf16[1024,4096]{1,0:T(8,128)(2,1)} %all-gather.5.cloned.1.call-done, bf16[1024,2048]{1,0:T(8,128)(2,1)} %all-gather.7.cloned.1.call-done), kind=kOutput, calls=%fused_computation.4 | convolution fusion | flops 17188257792 | bytes 79691776 | tf_op jit(solution)/shard_map/dot_general | solution.py:44
  209.6 65.1 %fusion.43 = f32[4096,512]{1,0:T(8,128)} fusion(f32[4096,2048]{1,0:T(8,128)} %convolution_add_fusion, f32[2048,512]{1,0:T(8,128)} %all-gather.9.cloned.1.call-done), kind=kOutput, calls=%fused_computation.85 | convolution fusion | flops 51539607552 | bytes 46137344 | tf_op jit(solution)/shard_map/dot_general | solution.py:52
  275.0 267.8 %all-reduce.4.cloned.1.call-done = f32[4096,512]{1,0:T(8,128)} async-done(((f32[4096,512]{1,0:T(8,128)}), f32[4096,512]{1,0:T(8,128)}) %all-reduce.4.cloned.1.call-update) | async-done | bytes 8388624 | tf_op jit(solution)/shard_map/psum | solution.py:55
  542.8 18.5 %fusion.44 = f32[512,512]{0,1:T(8,128)} fusion(f32[4096,512]{1,0:T(8,128)} %all-reduce.4.cloned.1.call-done), kind=kOutput, calls=%fused_computation.86 | convolution fusion | flops 12884901888 | bytes 9437184 | tf_op jit(solution)/shard_map/dot_general | solution.py:16
  562.3 34.6 %all-reduce.6.cloned.1.call-done = f32[512,512]{0,1:T(8,128)} async-done(((f32[512,512]{0,1:T(8,128)}), f32[512,512]{0,1:T(8,128)}) %all-reduce.6.cloned.1.call-update) | async-done | bytes 1048592 | tf_op jit(solution)/shard_map/psum | solution.py:56
  596.9 1.6 copy.9
  598.4 1.4 fusion.10
  599.9 11.7 %cholesky.104 = f32[128,128]{1,0:T(8,128)S(1)} custom-call(f32[128,128]{1,0:T(8,128)S(1)} %cholesky.266), custom_call_target="Cholesky" | custom-call | tf_op jit(solution)/shard_map/jit(cholesky)/cholesky | solution.py:36
  611.7 9.8 custom-call.31
  622.3 11.7 %cholesky.217 = f32[128,128]{1,0:T(8,128)S(1)} custom-call(f32[128,128]{1,0:T(8,128)S(1)} %cholesky.270), custom_call_target="Cholesky" | custom-call | tf_op jit(solution)/shard_map/jit(cholesky)/cholesky | solution.py:36
  634.0 18.5 %custom-call.32 = f32[1,128,128]{1,2,0:T(8,128)S(1)} custom-call(f32[1,128,128]{2,1,0:T(8,128)S(1)} %get-tuple-element.27), custom_call_target="InvertDiagBlocksLowerTriangular" | custom-call | tf_op jit(solution)/shard_map/jit(cholesky)/cholesky | solution.py:36
  653.2 11.7 %cholesky.238 = f32[128,128]{1,0:T(8,128)S(1)} custom-call(f32[128,128]{1,0:T(8,128)S(1)} %cholesky.275), custom_call_target="Cholesky" | custom-call | tf_op jit(solution)/shard_map/jit(cholesky)/cholesky | solution.py:36
  665.6 9.8 custom-call.33
  676.0 11.7 %cholesky.255 = f32[128,128]{1,0:T(8,128)S(1)} custom-call(f32[128,128]{1,0:T(8,128)S(1)} %convolution_subtract_fusion.5), custom_call_target="Cholesky" | custom-call | tf_op jit(solution)/shard_map/jit(cholesky)/cholesky | solution.py:36
  692.0 10.1 while.1
  692.6 1.9 bitcast_dynamic-update-slice_fusion.2
  695.1 1.9 bitcast_dynamic-update-slice_fusion.2
  697.6 1.9 bitcast_dynamic-update-slice_fusion.2
  700.2 1.9 bitcast_dynamic-update-slice_fusion.2
  702.1 40.1 %custom-call.34 = f32[4,128,128]{1,2,0:T(8,128)S(1)} custom-call(f32[4,128,128]{2,1,0:T(8,128)} %get-tuple-element.10), custom_call_target="InvertDiagBlocksLowerTriangular" | custom-call | tf_op jit(solution)/shard_map/jit(_solve_triangular)/triangular_solve | solution.py:38
  742.2 1.1 fusion.21
  746.0 17.1 %fusion.2 = f32[4096,512]{1,0:T(8,128)S(1)} fusion(f32[4096,512]{1,0:T(8,128)} %all-reduce.4.cloned.1.call-done, f32[128,512]{1,0:T(8,128)S(1)} %fusion.30, f32[128,512]{1,0:T(8,128)S(1)} %fusion.31, f32[128,512]{1,0:T(8,128)S(1)} %fusion.33, f32[128,512]{1,0:T(8,128)S(1)} %fusion.21), kind=kOutput, calls=%fused_computation.16 | convolution fusion | flops 12885688320 | bytes 17825792 | tf_op jit(solution)/shard_map/dot_general | solution.py:26
  763.2 3.2 copy-done
  766.4 58.7 %fusion.45 = f32[2048,512]{1,0:T(8,128)} fusion(f32[4096,2048]{1,0:T(8,128)} %convolution_add_fusion, f32[4096,512]{1,0:T(8,128)S(1)} %fusion.2), kind=kOutput, calls=%fused_computation.87 | convolution fusion | flops 51539607552 | bytes 46137344 | tf_op jit(solution)/shard_map/dot_general | solution.py:16
  825.2 45.2 %reduce-scatter.2.cloned.1.call-done = f32[512,512]{1,0:T(8,128)} async-done(((f32[2048,512]{1,0:T(8,128)}), f32[512,512]{1,0:T(8,128)}) %reduce-scatter.2.cloned.1.call-update) | async-done | bytes 1048592 | tf_op jit(solution)/shard_map/reduce_scatter | solution.py:58
  870.4 1.3 multiply_reduce_fusion
  871.7 39.7 %psum.23 = f32[512]{0:T(512)S(1)} all-reduce(f32[512]{0:T(512)S(1)} %multiply_reduce_fusion), channel_id=1, replica_groups=mesh['row'=4,'col'=8] {'row','col'}, use_global_device_ids=true, to_apply=%region_12.13 | all-reduce | flops 512 | bytes 4096 | tf_op jit(solution)/shard_map/psum | solution.py:61
  911.4 2.3 broadcast_divide_fusion
  913.8 62.5 %multiply_subtract_fusion = f32[4096,2048]{1,0:T(8,128)} fusion(f32[4096,2048]{1,0:T(8,128)} %convolution_add_fusion, f32[4096,512]{1,0:T(8,128)} %copy-done, f32[2048,512]{1,0:T(8,128)} %all-gather.11.cloned.1.call-done), kind=kOutput, calls=%fused_computation.2 | convolution fusion | flops 51556384768 | bytes 79691776 | tf_op jit(solution)/shard_map/dot_general | solution.py:26
  976.3 59.6 %subtract_convert_fusion = bf16[4096,2048]{1,0:T(8,128)(2,1)} fusion(bf16[4096,2048]{1,0:T(8,128)(2,1)} %param.5, f32[4096,512]{1,0:T(8,128)} %copy-done, f32[2048,512]{1,0:T(8,128)S(1)} %copy-done.1, f32[512]{0:T(512)S(1)} %add_sqrt_fusion), kind=kOutput, calls=%fused_computation.3 | convolution fusion | flops 51574210560 | bytes 46139392 | tf_op jit(solution)/shard_map/dot_general | solution.py:26
  (57 shorter events, 13.2 us)
Async XLA Ops:
  7.2 39.6 %all-gather.7.cloned.1.call-start = ((), (), s32[]{:S(2)}) async-start(), calls=%async_computation.2 | async-start | bytes 5242880 | tf_op jit(solution)/shard_map/all_gather | solution.py:46
  7.9 165.5 %all-gather.5.cloned.1.call-start = ((), (), s32[]{:S(2)}) async-start(), calls=%async_computation.1 | async-start | bytes 9437184 | tf_op jit(solution)/shard_map/all_gather | solution.py:43
  8.6 201.0 %all-gather.9.cloned.1.call-start = ((), (), s32[]{:S(2)}) async-start(), calls=%async_computation.3 | async-start | bytes 5242880 | tf_op jit(solution)/shard_map/all_gather | solution.py:51
  9.4 533.4 %all-reduce.4.cloned.1.call-start = ((), (), s32[]{:S(2)}) async-start(), calls=%async_computation.4 | async-start | bytes 16777216 | tf_op jit(solution)/shard_map/psum | solution.py:55
  274.7 322.2 %all-reduce.6.cloned.1.call-start = ((), (), s32[]{:S(2)}) async-start(), calls=%async_computation.5 | async-start | bytes 2097152 | tf_op jit(solution)/shard_map/psum | solution.py:56
  561.3 309.0 %reduce-scatter.2.cloned.1.call-start = ((), (), s32[]{:S(2)}) async-start(), calls=%async_computation.6 | async-start | bytes 5242880 | tf_op jit(solution)/shard_map/reduce_scatter | solution.py:58
  763.2 3.2 copy-start
  825.1 88.6 %all-gather.11.cloned.1.call-start = ((), (), s32[]{:S(2)}) async-start(), calls=%async_computation.7 | async-start | bytes 5242880 | tf_op jit(solution)/shard_map/all_gather | solution.py:64
  913.8 62.5 %copy-start.1 = (f32[2048,512]{1,0:T(8,128)S(1)}, f32[2048,512]{1,0:T(8,128)}, u32[]{:S(2)}) copy-start(f32[2048,512]{1,0:T(8,128)} %all-gather.11.cloned.1.call-done) | copy-start | bytes 12582916
Sparse Core Ops, SparseCore 0:
  9.5 37.1 all-gather.6
  48.9 124.4 all-gather.4
  174.9 32.6 all-gather.8
  274.8 267.9 all-reduce.3
  561.5 35.3 all-reduce.5
  825.3 45.0 reduce-scatter.1
  871.9 34.7 all-gather.10
where the time goes:
time: 1050 us; the launch traced here: 1040 us
  waiting for transfers between devices  514 us (49%)
  matrix products  323 us (31%)
  other arithmetic  134 us (13%)
  blocking collectives  39.7 us (4%)
  between operations  17.2 us (2%)
  local copies, waits for them, and re-layouts  15 us (1%)
    psum x1, waiting for transfers between devices, body(): left_factor = lax.psum(left_partial, 'col')  268 us
    dot_general x3, matrix products, outer_rows(): lax.dot_general(first, second, (((1,), (1,)), ((), ())), precision=FULL_P...  139 us
    all_gather x1, waiting for transfers between devices, body(): grads_whole = lax.all_gather(output_grads, 'col', axis=0, tiled=True)  127 us
    another operation x14, other arithmetic, orthogonalize(): lower_factor = jnp.linalg.cholesky(gram_matrix)  87.4 us
    dot_general x2, matrix products, contract_rows(): lax.dot_general(first, second, (((0,), (0,)), ((), ())), precision=FULL_P...  77.2 us
    dot_general x1, matrix products, body(): jnp.dot(buffer, factor_block, precision=FULL_PRECISION, preferred_element...  65.1 us
    reduce_scatter x1, waiting for transfers between devices, body(): lax.psum_scatter(contract_rows(buffer, ortho_left), 'row', scatter_dimens...  45.2 us
    another operation x3, other arithmetic, orthogonalize(): jax.scipy.linalg.solve_triangular(lower_factor, identity, lower=True)  40.3 us
  transfers between devices with their start and end apart: 7, of which 5 were waited for; matrix products, arithmetic and copies ran while one was open for 4% of the time, Pallas kernels for 0%

commit v1 on v0

--- a/solution.py
+++ b/solution.py
@@ -40,7 +40,13 @@
 
 
 def body(weight, momentum, right_factor, output_grads, activations):
-    grads_whole = lax.all_gather(output_grads, "col", axis=0, tiled=True)
+    size = lax.axis_size("col")
+    block, shards = (output_grads, [output_grads])
+    for _ in range(size - 1):
+        block = lax.ppermute(block, "col", [(i, (i + 1) % size) for i in range(size)])
+        shards.insert(0, block)
+    flat = jnp.concatenate(shards, axis=0)
+    grads_whole = jnp.roll(flat, (lax.axis_index("col") + 1) * output_grads.shape[0], axis=0)
     grad_tile = lax.dot_general(
         grads_whole,
         lax.all_gather(activations, "row", axis=0, tiled=True),

time: 1050 us -> 1090 us (1.038)
  local copies, waits for them, and re-layouts: 15 us -> 43.3 us
    ppermute x0 -> x7, waiting for transfers between devices: none -> 176 us  [body(): lax.ppermute(block, 'col', [(i, (i + 1) % size) for i in range(size)])]
    all_gather x1 -> x0, waiting for transfers between devices: 127 us -> none  [body(): grads_whole = lax.all_gather(output_grads, 'col', axis=0, tiled=True)]
    all_gather x1, waiting for transfers between devices: 37.3 us -> 0.01 us  [body(): lax.all_gather(activations, 'row', axis=0, tiled=True)]
    unnamed x4 -> x33, local copies, waits for them, and re-layouts: 3.22 us -> 30.6 us
  transfers between devices with their start and end apart: 7 -> 13, of which waited for: 5 -> 10; matrix products, arithmetic and copies ran while one was open for 4% -> 6% of each run, Pallas kernels for 0% -> 0%
where the time goes in v1:
time: 1090 us; the launch traced here: 1080 us
  waiting for transfers between devices  522 us (48%)
  matrix products  323 us (30%)
  other arithmetic  134 us (12%)
  local copies, waits for them, and re-layouts  43.3 us (4%)
  blocking collectives  39.7 us (4%)
  between operations  17.4 us (2%)
    psum x1, waiting for transfers between devices, body(): left_factor = lax.psum(left_partial, 'col')  266 us
    ppermute x7, waiting for transfers between devices, body(): lax.ppermute(block, 'col', [(i, (i + 1) % size) for i in range(size)])  176 us
    dot_general x3, matrix products, outer_rows(): lax.dot_general(first, second, (((1,), (1,)), ((), ())), precision=FULL_P...  139 us
    another operation x14, other arithmetic, orthogonalize(): lower_factor = jnp.linalg.cholesky(gram_matrix)  87.5 us
    dot_general x2, matrix products, contract_rows(): lax.dot_general(first, second, (((0,), (0,)), ((), ())), precision=FULL_P...  77.1 us
    dot_general x1, matrix products, body(): jnp.dot(buffer, factor_block, precision=FULL_PRECISION, preferred_element...  65.1 us
    reduce_scatter x1, waiting for transfers between devices, body(): lax.psum_scatter(contract_rows(buffer, ortho_left), 'row', scatter_dimens...  45.2 us
    another operation x3, other arithmetic, orthogonalize(): jax.scipy.linalg.solve_triangular(lower_factor, identity, lower=True)  40.3 us
  transfers between devices with their start and end apart: 13, of which 10 were waited for; matrix products, arithmetic and copies ran while one was open for 6% of the time, Pallas kernels for 0%

profile of v1, /device:TPU:0, one launch (start us, length us, event | category | flops | bytes accessed | tf_op | source)
XLA Modules:
  0.0 1082.5 jit_solution(17393228142728730800)
XLA Ops:
  7.2 3.0 collective-permute-start
  10.3 26.3 %collective-permute-done = bf16[128,4096]{1,0:T(8,128)(2,1)S(1)} collective-permute-done((bf16[128,4096]{1,0:T(8,128)(2,1)}, bf16[128,4096]{1,0:T(8,128)(2,1)S(1)}, u32[]{:S(2)}, u32[]{:S(2)}) %collective-permute-start) | collective-permute-done | bytes 1048608 | tf_op jit(solution)/shard_map/ppermute | solution.py:46
  36.7 27.0 %collective-permute-done.1 = bf16[128,4096]{1,0:T(8,128)(2,1)S(1)} collective-permute-done((bf16[128,4096]{1,0:T(8,128)(2,1)S(1)}, bf16[128,4096]{1,0:T(8,128)(2,1)S(1)}, u32[]{:S(2)}, u32[]{:S(2)}) %collective-permute-start.1) | collective-permute-done | bytes 1048608 | tf_op jit(solution)/shard_map/ppermute | solution.py:46
  63.7 26.2 %collective-permute-done.2 = bf16[128,4096]{1,0:T(8,128)(2,1)S(1)} collective-permute-done((bf16[128,4096]{1,0:T(8,128)(2,1)S(1)}, bf16[128,4096]{1,0:T(8,128)(2,1)S(1)}, u32[]{:S(2)}, u32[]{:S(2)}) %collective-permute-start.2) | collective-permute-done | bytes 1048608 | tf_op jit(solution)/shard_map/ppermute | solution.py:46
  90.9 25.3 %collective-permute-done.3 = bf16[128,4096]{1,0:T(8,128)(2,1)S(1)} collective-permute-done((bf16[128,4096]{1,0:T(8,128)(2,1)S(1)}, bf16[128,4096]{1,0:T(8,128)(2,1)S(1)}, u32[]{:S(2)}, u32[]{:S(2)}) %collective-permute-start.3) | collective-permute-done | bytes 1048608 | tf_op jit(solution)/shard_map/ppermute | solution.py:46
  117.2 24.4 %collective-permute-done.4 = bf16[128,4096]{1,0:T(8,128)(2,1)S(1)} collective-permute-done((bf16[128,4096]{1,0:T(8,128)(2,1)S(1)}, bf16[128,4096]{1,0:T(8,128)(2,1)S(1)}, u32[]{:S(2)}, u32[]{:S(2)}) %collective-permute-start.4) | collective-permute-done | bytes 1048608 | tf_op jit(solution)/shard_map/ppermute | solution.py:46
  142.6 23.7 %collective-permute-done.5 = bf16[128,4096]{1,0:T(8,128)(2,1)} collective-permute-done((bf16[128,4096]{1,0:T(8,128)(2,1)S(1)}, bf16[128,4096]{1,0:T(8,128)(2,1)}, u32[]{:S(2)}, u32[]{:S(2)}) %collective-permute-start.5) | collective-permute-done | bytes 1048608 | tf_op jit(solution)/shard_map/ppermute | solution.py:46
  166.5 22.9 %collective-permute-done.6 = bf16[128,4096]{1,0:T(8,128)(2,1)} collective-permute-done((bf16[128,4096]{1,0:T(8,128)(2,1)}, bf16[128,4096]{1,0:T(8,128)(2,1)}, u32[]{:S(2)}, u32[]{:S(2)}) %collective-permute-start.6) | collective-permute-done | bytes 1048608 | tf_op jit(solution)/shard_map/ppermute | solution.py:46
  189.4 2.3 constant_dynamic-update-slice_fusion.15
  191.7 2.3 constant_dynamic-update-slice_fusion.14
  214.8 36.0 %convolution_add_fusion = f32[4096,2048]{1,0:T(8,128)} fusion(f32[4096,2048]{1,0:T(8,128)} %param.6, bf16[1024,2048]{1,0:T(8,128)(2,1)} %all-gather.4.cloned.1.call-done, bf16[2048,4096]{1,0:T(8,128)(2,1)} %constant_dynamic-update-slice_fusion, s32[]{:T(128)S(6)} %select_n.18), kind=kOutput, calls=%fused_computation.4 | convolution fusion | flops 17188257792 | bytes 79691776 | tf_op jit(solution)/shard_map/dot_general | solution.py:50
  250.8 65.1 %fusion.45 = f32[4096,512]{1,0:T(8,128)} fusion(f32[4096,2048]{1,0:T(8,128)} %convolution_add_fusion, f32[2048,512]{1,0:T(8,128)} %all-gather.6.cloned.1.call-done), kind=kOutput, calls=%fused_computation.103 | convolution fusion | flops 51539607552 | bytes 46137344 | tf_op jit(solution)/shard_map/dot_general | solution.py:58
  316.2 266.1 %all-reduce.4.cloned.1.call-done = f32[4096,512]{1,0:T(8,128)} async-done(((f32[4096,512]{1,0:T(8,128)}), f32[4096,512]{1,0:T(8,128)}) %all-reduce.4.cloned.1.call-update) | async-done | bytes 8388624 | tf_op jit(solution)/shard_map/psum | solution.py:61
  582.3 18.3 %fusion.46 = f32[512,512]{0,1:T(8,128)} fusion(f32[4096,512]{1,0:T(8,128)} %all-reduce.4.cloned.1.call-done), kind=kOutput, calls=%fused_computation.104 | convolution fusion | flops 12884901888 | bytes 9437184 | tf_op jit(solution)/shard_map/dot_general | solution.py:16
  601.6 34.6 %all-reduce.6.cloned.1.call-done = f32[512,512]{0,1:T(8,128)} async-done(((f32[512,512]{0,1:T(8,128)}), f32[512,512]{0,1:T(8,128)}) %all-reduce.6.cloned.1.call-update) | async-done | bytes 1048592 | tf_op jit(solution)/shard_map/psum | solution.py:62
  639.2 11.7 %cholesky.104 = f32[128,128]{1,0:T(8,128)S(1)} custom-call(f32[128,128]{1,0:T(8,128)S(1)} %cholesky.266), custom_call_target="Cholesky" | custom-call | tf_op jit(solution)/shard_map/jit(cholesky)/cholesky | solution.py:36
  651.0 9.8 custom-call.31
  661.6 11.7 %cholesky.217 = f32[128,128]{1,0:T(8,128)S(1)} custom-call(f32[128,128]{1,0:T(8,128)S(1)} %cholesky.270), custom_call_target="Cholesky" | custom-call | tf_op jit(solution)/shard_map/jit(cholesky)/cholesky | solution.py:36
  673.3 18.5 %custom-call.32 = f32[1,128,128]{1,2,0:T(8,128)S(1)} custom-call(f32[1,128,128]{2,1,0:T(8,128)S(1)} %get-tuple-element.27), custom_call_target="InvertDiagBlocksLowerTriangular" | custom-call | tf_op jit(solution)/shard_map/jit(cholesky)/cholesky | solution.py:36
  692.5 11.7 %cholesky.238 = f32[128,128]{1,0:T(8,128)S(1)} custom-call(f32[128,128]{1,0:T(8,128)S(1)} %cholesky.275), custom_call_target="Cholesky" | custom-call | tf_op jit(solution)/shard_map/jit(cholesky)/cholesky | solution.py:36
  704.9 9.8 custom-call.33
  715.3 11.7 %cholesky.255 = f32[128,128]{1,0:T(8,128)S(1)} custom-call(f32[128,128]{1,0:T(8,128)S(1)} %convolution_subtract_fusion.5), custom_call_target="Cholesky" | custom-call | tf_op jit(solution)/shard_map/jit(cholesky)/cholesky | solution.py:36
  731.5 10.0 while.1
  741.5 40.1 %custom-call.34 = f32[4,128,128]{1,2,0:T(8,128)S(1)} custom-call(f32[4,128,128]{2,1,0:T(8,128)} %get-tuple-element.10), custom_call_target="InvertDiagBlocksLowerTriangular" | custom-call | tf_op jit(solution)/shard_map/jit(_solve_triangular)/triangular_solve | solution.py:38
  785.4 17.1 %fusion.3 = f32[4096,512]{1,0:T(8,128)S(1)} fusion(f32[4096,512]{1,0:T(8,128)} %all-reduce.4.cloned.1.call-done, f32[128,512]{1,0:T(8,128)S(1)} %fusion.31, f32[128,512]{1,0:T(8,128)S(1)} %fusion.32, f32[128,512]{1,0:T(8,128)S(1)} %fusion.34, f32[128,512]{1,0:T(8,128)S(1)} %fusion.22), kind=kOutput, calls=%fused_computation.17 | convolution fusion | flops 12885688320 | bytes 17825792 | tf_op jit(solution)/shard_map/dot_general | solution.py:26
  802.6 3.2 copy-done
  805.8 58.7 %fusion.47 = f32[2048,512]{1,0:T(8,128)} fusion(f32[4096,2048]{1,0:T(8,128)} %convolution_add_fusion, f32[4096,512]{1,0:T(8,128)S(1)} %fusion.3), kind=kOutput, calls=%fused_computation.105 | convolution fusion | flops 51539607552 | bytes 46137344 | tf_op jit(solution)/shard_map/dot_general | solution.py:16
  864.6 45.2 %reduce-scatter.2.cloned.1.call-done = f32[512,512]{1,0:T(8,128)} async-done(((f32[2048,512]{1,0:T(8,128)}), f32[512,512]{1,0:T(8,128)}) %reduce-scatter.2.cloned.1.call-update) | async-done | bytes 1048592 | tf_op jit(solution)/shard_map/reduce_scatter | solution.py:64
  911.1 39.7 %psum.23 = f32[512]{0:T(512)S(1)} all-reduce(f32[512]{0:T(512)S(1)} %multiply_reduce_fusion), channel_id=1, replica_groups=mesh['row'=4,'col'=8] {'row','col'}, use_global_device_ids=true, to_apply=%region_12.13 | all-reduce | flops 512 | bytes 4096 | tf_op jit(solution)/shard_map/psum | solution.py:67
  950.8 2.3 broadcast_divide_fusion
  953.1 62.5 %multiply_subtract_fusion = f32[4096,2048]{1,0:T(8,128)} fusion(f32[4096,2048]{1,0:T(8,128)} %convolution_add_fusion, f32[4096,512]{1,0:T(8,128)} %copy-done, f32[2048,512]{1,0:T(8,128)} %all-gather.8.cloned.1.call-done), kind=kOutput, calls=%fused_computation.2 | convolution fusion | flops 51556384768 | bytes 79691776 | tf_op jit(solution)/shard_map/dot_general | solution.py:26
  1015.6 59.6 %subtract_convert_fusion = bf16[4096,2048]{1,0:T(8,128)(2,1)} fusion(bf16[4096,2048]{1,0:T(8,128)(2,1)} %param.5, f32[4096,512]{1,0:T(8,128)} %copy-done, f32[2048,512]{1,0:T(8,128)S(1)} %copy-done.1, f32[512]{0:T(512)S(1)} %add_sqrt_fusion), kind=kOutput, calls=%fused_computation.3 | convolution fusion | flops 51574210560 | bytes 46139392 | tf_op jit(solution)/shard_map/dot_general | solution.py:26
  (98 shorter events, 48.1 us)
Async XLA Ops:
  7.2 195.8 %copy-start.2 = (bf16[128,4096]{1,0:T(8,128)(2,1)S(1)}, bf16[128,4096]{1,0:T(8,128)(2,1)}, u32[]{:S(2)}) copy-start(bf16[128,4096]{1,0:T(8,128)(2,1)} %param.8) | copy-start | bytes 3145732
  7.2 207.6 %all-gather.4.cloned.1.call-start = ((), (), s32[]{:S(2)}) async-start(), calls=%async_computation.1 | async-start | bytes 5242880 | tf_op jit(solution)/shard_map/all_gather | solution.py:52
  7.2 29.5 %collective-permute-start = (bf16[128,4096]{1,0:T(8,128)(2,1)}, bf16[128,4096]{1,0:T(8,128)(2,1)S(1)}, u32[]{:S(2)}, u32[]{:S(2)}) collective-permute-start(bf16[128,4096]{1,0:T(8,128)(2,1)} %param.8), channel_id=1, source_target_pairs={{0,1},{1,2},{2,3},{3,4},{4,5},{5,6},{6,7},{7,0},{8,9},{9,10},{10,1... | collective-permute-start | bytes 3145736 | tf_op jit(solution)/shard_map/ppermute | solution.py:46
  10.3 240.5 %all-gather.6.cloned.1.call-start = ((), (), s32[]{:S(2)}) async-start(), calls=%async_computation.2 | async-start | bytes 5242880 | tf_op jit(solution)/shard_map/all_gather | solution.py:57
  36.7 27.0 %collective-permute-start.1 = (bf16[128,4096]{1,0:T(8,128)(2,1)S(1)}, bf16[128,4096]{1,0:T(8,128)(2,1)S(1)}, u32[]{:S(2)}, u32[]{:S(2)}) collective-permute-start(bf16[128,4096]{1,0:T(8,128)(2,1)S(1)} %collective-permute-done), channel_id=1, source_target_pairs={{0,1},{1,2},{2,3},{3,4},{4,5},{5,6},{6,7},{7,0},{8,9},{9,10},{10,1... | collective-permute-start | bytes 3145736 | tf_op jit(solution)/shard_map/ppermute | solution.py:46
  63.7 26.2 %collective-permute-start.2 = (bf16[128,4096]{1,0:T(8,128)(2,1)S(1)}, bf16[128,4096]{1,0:T(8,128)(2,1)S(1)}, u32[]{:S(2)}, u32[]{:S(2)}) collective-permute-start(bf16[128,4096]{1,0:T(8,128)(2,1)S(1)} %collective-permute-done.1), channel_id=1, source_target_pairs={{0,1},{1,2},{2,3},{3,4},{4,5},{5,6},{6,7},{7,0},{8,9},{9,10},{10,1... | collective-permute-start | bytes 3145736 | tf_op jit(solution)/shard_map/ppermute | solution.py:46
  89.9 1.1 copy-start.3
  90.9 25.3 %collective-permute-start.3 = (bf16[128,4096]{1,0:T(8,128)(2,1)S(1)}, bf16[128,4096]{1,0:T(8,128)(2,1)S(1)}, u32[]{:S(2)}, u32[]{:S(2)}) collective-permute-start(bf16[128,4096]{1,0:T(8,128)(2,1)S(1)} %collective-permute-done.2), channel_id=1, source_target_pairs={{0,1},{1,2},{2,3},{3,4},{4,5},{5,6},{6,7},{7,0},{8,9},{9,10},{10,1... | collective-permute-start | bytes 3145736 | tf_op jit(solution)/shard_map/ppermute | solution.py:46
  116.2 1.0 copy-start.5
  117.2 24.5 %collective-permute-start.4 = (bf16[128,4096]{1,0:T(8,128)(2,1)S(1)}, bf16[128,4096]{1,0:T(8,128)(2,1)S(1)}, u32[]{:S(2)}, u32[]{:S(2)}) collective-permute-start(bf16[128,4096]{1,0:T(8,128)(2,1)S(1)} %collective-permute-done.3), channel_id=1, source_target_pairs={{0,1},{1,2},{2,3},{3,4},{4,5},{5,6},{6,7},{7,0},{8,9},{9,10},{10,1... | collective-permute-start | bytes 3145736 | tf_op jit(solution)/shard_map/ppermute | solution.py:46
  141.6 1.0 copy-start.7
  142.6 23.7 %collective-permute-start.5 = (bf16[128,4096]{1,0:T(8,128)(2,1)S(1)}, bf16[128,4096]{1,0:T(8,128)(2,1)}, u32[]{:S(2)}, u32[]{:S(2)}) collective-permute-start(bf16[128,4096]{1,0:T(8,128)(2,1)S(1)} %collective-permute-done.4), channel_id=1, source_target_pairs={{0,1},{1,2},{2,3},{3,4},{4,5},{5,6},{6,7},{7,0},{8,9},{9,10},{10,1... | collective-permute-start | bytes 3145736 | tf_op jit(solution)/shard_map/ppermute | solution.py:46
  166.3 23.1 %collective-permute-start.6 = (bf16[128,4096]{1,0:T(8,128)(2,1)}, bf16[128,4096]{1,0:T(8,128)(2,1)}, u32[]{:S(2)}, u32[]{:S(2)}) collective-permute-start(bf16[128,4096]{1,0:T(8,128)(2,1)} %collective-permute-done.5), channel_id=1, source_target_pairs={{0,1},{1,2},{2,3},{3,4},{4,5},{5,6},{6,7},{7,0},{8,9},{9,10},{10,1... | collective-permute-start | bytes 3145736 | tf_op jit(solution)/shard_map/ppermute | solution.py:46
  166.3 415.9 %all-reduce.4.cloned.1.call-start = ((), (), s32[]{:S(2)}) async-start(), calls=%async_computation.3 | async-start | bytes 16777216 | tf_op jit(solution)/shard_map/psum | solution.py:61
  166.4 42.1 %copy-start.8 = (bf16[128,4096]{1,0:T(8,128)(2,1)S(1)}, bf16[128,4096]{1,0:T(8,128)(2,1)}, u32[]{:S(2)}) copy-start(bf16[128,4096]{1,0:T(8,128)(2,1)} %copy-done.7) | copy-start | bytes 3145732
  166.4 43.2 %copy-start.6 = (bf16[128,4096]{1,0:T(8,128)(2,1)S(1)}, bf16[128,4096]{1,0:T(8,128)(2,1)}, u32[]{:S(2)}) copy-start(bf16[128,4096]{1,0:T(8,128)(2,1)} %copy-done.5) | copy-start | bytes 3145732
  166.4 44.2 %copy-start.4 = (bf16[128,4096]{1,0:T(8,128)(2,1)S(1)}, bf16[128,4096]{1,0:T(8,128)(2,1)}, u32[]{:S(2)}) copy-start(bf16[128,4096]{1,0:T(8,128)(2,1)} %copy-done.3) | copy-start | bytes 3145732
  315.9 320.3 %all-reduce.6.cloned.1.call-start = ((), (), s32[]{:S(2)}) async-start(), calls=%async_computation.4 | async-start | bytes 2097152 | tf_op jit(solution)/shard_map/psum | solution.py:62
  600.6 309.1 %reduce-scatter.2.cloned.1.call-start = ((), (), s32[]{:S(2)}) async-start(), calls=%async_computation.5 | async-start | bytes 5242880 | tf_op jit(solution)/shard_map/reduce_scatter | solution.py:64
  802.5 3.2 copy-start
  864.5 88.6 %all-gather.8.cloned.1.call-start = ((), (), s32[]{:S(2)}) async-start(), calls=%async_computation.6 | async-start | bytes 5242880 | tf_op jit(solution)/shard_map/all_gather | solution.py:70
  953.1 62.5 %copy-start.1 = (f32[2048,512]{1,0:T(8,128)S(1)}, f32[2048,512]{1,0:T(8,128)}, u32[]{:S(2)}) copy-start(f32[2048,512]{1,0:T(8,128)} %all-gather.8.cloned.1.call-done) | copy-start | bytes 12582916
Sparse Core Ops, SparseCore 0:
  10.4 36.2 all-gather.3
  166.5 35.0 all-gather.5
  316.0 266.2 all-reduce.3
  600.8 35.3 all-reduce.5
  864.7 45.0 reduce-scatter.1
  911.2 34.7 all-gather.7
